TPU v7x, 8 devices: a whole 2x2x1 slice. The times are simulated.
8 devices in a mesh: dp: 2 (over z, y), tp: 4 (over x, core).
Axes of the slice: x: 2, y: 2, z: 1, core: 2. Of those that a mesh axis runs over, the one named last changes fastest.
Arguments:
- hidden: bfloat16 [256, 512], P(('dp', 'tp')), parts along dimension 0
- ln_gain: float32 [512], replicated
- ln_bias: float32 [512], replicated
- out_embed: bfloat16 [50688, 512], P('tp')
- vocab_valid: int32 [50688], P('tp')
- targets: int32 [256], P(('dp', 'tp')), parts along dimension 0
- loss_mask: int32 [256], P(('dp', 'tp')), parts along dimension 0
Outputs:
- output 1: float32 [256], P(('dp', 'tp')), parts along dimension 0
- output 2: float32 [2], P('dp'), parts along dimension 0
- output 3: bfloat16 [256, 512], P(('dp', 'tp')), parts along dimension 0
- output 4: float32 [101376, 512], P(('dp', 'tp')), parts along dimension 0
- output 5: float32 [1024], P('dp'), parts along dimension 0
- output 6: float32 [1024], P('dp'), parts along dimension 0
There are 2 independent parts. A program takes and returns all parts, laid end to end along the dimension named above; an argument that names none is the same for every part.
All inputs are finite; a program needn't handle non-finite values.
Results may differ from a plain program's by a relative error of at most 0.001.
Values are sent between devices in bfloat16 or wider.
A program may use at most 1 GiB of HBM per device.

v0:
```python
import jax
import jax.numpy as jnp
from jax import lax
from jax.sharding import PartitionSpec as P

SOFT_CAP = 30.0
Z_COEF = 1e-4
LN_EPS = 1e-5


def layer_norm(h_float, ln_gain, ln_bias):
    mean_val = jnp.mean(h_float, axis=-1, keepdims=True)
    centered = h_float - mean_val
    var_val = jnp.mean(centered * centered, axis=-1, keepdims=True)
    return centered * lax.rsqrt(var_val + LN_EPS) * ln_gain + ln_bias


def solution(mesh):
    def group_step(hidden, ln_gain, ln_bias, out_embed, vocab_valid, targets, loss_mask):
        rows_loc = hidden.shape[0]
        vocab_loc = out_embed.shape[0]
        shard_idx = lax.axis_index("tp")
        normed, ln_back = jax.vjp(layer_norm, hidden.astype(jnp.float32), ln_gain, ln_bias)
        x_all = lax.all_gather(normed.astype(jnp.bfloat16), "tp", axis=0, tiled=True)
        tgt_all = lax.all_gather(targets, "tp", axis=0, tiled=True)
        mask_all = lax.all_gather(loss_mask, "tp", axis=0, tiled=True).astype(jnp.float32)
        logits = lax.dot_general(x_all, out_embed, (((1,), (1,)), ((), ())), preferred_element_type=jnp.float32)
        tanh_val = jnp.tanh(logits / SOFT_CAP)
        capped = SOFT_CAP * tanh_val
        col_ok = (vocab_valid != 0)[None, :]
        masked = jnp.where(col_ok, capped, -SOFT_CAP)
        glob_max = lax.pmax(jnp.max(masked, axis=1), "tp")
        exp_vals = jnp.where(col_ok, jnp.exp(masked - glob_max[:, None]), 0.0)
        col_ids = shard_idx * vocab_loc + jnp.arange(vocab_loc)
        is_target = tgt_all[:, None] == col_ids[None, :]
        local_stats = jnp.stack([jnp.sum(exp_vals, axis=1), jnp.sum(jnp.where(is_target, capped, 0.0), axis=1)])
        group_stats = lax.psum(local_stats, "tp")
        sum_exp = group_stats[0]
        lse = glob_max + jnp.log(sum_exp)
        tok_count = jnp.sum(mask_all)
        loss_all = (lse - group_stats[1] + Z_COEF * lse * lse) * mask_all
        mean_loss = jnp.sum(loss_all) / tok_count
        tok_coef = mask_all / tok_count
        prob_coef = (1.0 + 2.0 * Z_COEF * lse) * tok_coef / sum_exp
        d_capped = prob_coef[:, None] * exp_vals - jnp.where(is_target, tok_coef[:, None], 0.0)
        d_logits = (d_capped * (1.0 - tanh_val * tanh_val)).astype(jnp.bfloat16)
        d_embed = lax.dot_general(d_logits, x_all, (((0,), (0,)), ((), ())), preferred_element_type=jnp.float32)
        dx_part = jnp.dot(d_logits, out_embed, preferred_element_type=jnp.float32)
        d_normed = lax.psum_scatter(dx_part, "tp", scatter_dimension=0, tiled=True)
        d_hidden, gain_part, bias_part = ln_back(d_normed)
        d_gain = lax.psum(gain_part, "tp")
        d_bias = lax.psum(bias_part, "tp")
        tok_loss = lax.dynamic_slice_in_dim(loss_all, shard_idx * rows_loc, rows_loc)
        return tok_loss, mean_loss.reshape(1), d_hidden.astype(jnp.bfloat16), d_embed, d_gain, d_bias

    row_spec = P(("dp", "tp"))
    mat_spec = P(("dp", "tp"), None)
    return jax.shard_map(group_step, mesh=mesh, in_specs=(mat_spec, P(None), P(None), P("tp", None), P("tp"), row_spec, row_spec), out_specs=(row_spec, P("dp"), mat_spec, mat_spec, P("dp"), P("dp")), check_vma=False)
```

profile of v0, /device:TPU:0, one launch (start us, length us, event | category | flops | bytes accessed | tf_op | source)
XLA Modules:
  0.0 107.0 jit_solution(7214717589626032307)
XLA Ops:
  7.2 0.0 reduce-scatter.2.cloned.1.call-start
  7.2 0.9 convert_reduce_fusion
  8.1 0.9 fusion.15
  9.1 1.2 %dynamic-slice = u32[1]{0:T(128)} dynamic-slice(u32[8]{0:T(128)} %constant.42, u32[]{:T(128)S(6)} %add.65), dynamic_slice_sizes={1} | dynamic-slice | bytes 12
  11.0 0.9 dynamic-update-slice.1
  11.8 0.8 dynamic-update-slice
  12.7 6.8 %all-reduce.2 = (s32[128]{0:T(128)S(1)}, s32[128]{0:T(128)S(1)}) all-reduce(s32[128]{0:T(128)S(1)} %dynamic-update-slice.1, s32[128]{0:T(128)S(1)} %dynamic-update-slice), channel_id=1, replica_groups=mesh['dp'=2,'tp'=4] {'tp'}, use_global_device_ids=true, to_apply=%add.1 | all-reduce | flops 256 | bytes 2048
  19.4 0.6 convert_reduce_fusion.1
  20.0 0.8 broadcast_compare_fusion
  20.9 0.9 fusion.13
  21.7 7.8 %all_gather.9 = bf16[128,512]{1,0:T(8,128)(2,1)S(1)} all-gather(bf16[32,512]{1,0:T(8,128)(2,1)S(1)} %fusion.13), channel_id=1, replica_groups=mesh['dp'=2,'tp'=4] {'tp'}, dimensions={0}, use_global_device_ids=true | all-gather | bytes 163840 | tf_op jit(solution)/shard_map/all_gather | solution.py:24
  29.5 11.8 %select_reduce_fusion = (f32[128]{0:T(128)S(1)}, f32[128,12672]{1,0:T(8,128)}) fusion(pred[12672]{0:T(1024)(128)(4,1)S(1)} %broadcast_compare_fusion, bf16[128,512]{1,0:T(8,128)(2,1)S(1)} %all_gather.9, bf16[12672,512]{1,0:T(8,128)(2,1)} %param.10), kind=kOutput, calls=%fused_computation.9 | convolution fusion | flops 1667432320 | bytes 19608448 | tf_op jit(solution)/shard_map/dot_general | solution.py:27
  41.3 5.6 %pmax.7 = f32[128]{0:T(128)S(1)} all-reduce(f32[128]{0:T(128)S(1)} %get-tuple-element.23), channel_id=1, replica_groups=mesh['dp'=2,'tp'=4] {'tp'}, use_global_device_ids=true, to_apply=%region_3.4 | all-reduce | flops 128 | bytes 1024 | tf_op jit(solution)/shard_map/pmax | solution.py:32
  46.9 5.3 %fusion.5 = (f32[128]{0:T(128)S(1)}, f32[128]{0:T(128)S(1)}) fusion(f32[128,12672]{1,0:T(8,128)} %get-tuple-element.24, f32[128]{0:T(128)S(1)} %pmax.7, pred[12672]{0:T(1024)(128)(4,1)S(1)} %broadcast_compare_fusion, s32[12672]{0:T(1024)S(1)} %iota_add_fusion, s32[128]{0:T(128)S(1)} %get-tuple-element.12), kind=kLoop, calls=%fused_computation.10 | loop fusion | flops 12975872 | bytes 6553472 | tf_op jit(solution)/shard_map/reduce_sum | solution.py:36
  52.2 6.7 %psum.21 = f32[2,128]{1,0:T(2,128)S(1)} all-reduce(f32[2,128]{1,0:T(2,128)S(1)} %pad_maximum_fusion), channel_id=1, replica_groups=mesh['dp'=2,'tp'=4] {'tp'}, use_global_device_ids=true, to_apply=%region_6.7 | all-reduce | flops 256 | bytes 2048 | tf_op jit(solution)/shard_map/psum | solution.py:37
  59.0 1.3 %bitcast_divide_fusion = (f32[128]{0:T(128)S(1)}, f32[128]{0:T(128)S(1)}, f32[]{:T(128)}, f32[128]{0:T(128)S(1)}) fusion(f32[2,128]{1,0:T(2,128)S(1)} %psum.21, f32[128]{0:T(128)S(1)} %pmax.7, f32[]{:T(128)} %convert_reduce_fusion.1, s32[128]{0:T(128)S(1)} %get-tuple-element.11), kind=kLoop, calls=%fused_computation.33 | loop fusion | flops 1663 | bytes 3592 | tf_op jit(solution)/shard_map/div | solution.py:44
  60.2 10.3 %fusion.23 = f32[128,512]{1,0:T(8,128)} fusion(bf16[12672,512]{1,0:T(8,128)(2,1)} %param.10, f32[128,12672]{1,0:T(8,128)} %get-tuple-element.24, f32[128]{0:T(128)S(1)} %get-tuple-element.18, f32[128]{0:T(128)S(1)} %get-tuple-element.17, s32[12672]{0:T(1024)S(1)} %iota_add_fusion, f32[128]{0:T(128)S(1)} %pmax.7, s32[128]{0:T(128)S(1)} %get-tuple-element.12, ...), kind=kOutput, calls=%fused_computation.44 | convolution fusion | flops 1680408576 | bytes 19791744 | tf_op jit(solution)/shard_map/dot_general | solution.py:48
  70.5 0.0 reduce-scatter.2.cloned.1.call-update
  70.6 0.0 copy-start
  70.6 0.0 copy-start.1
  70.6 17.5 %fusion.21 = f32[12672,512]{1,0:T(8,128)} fusion(bf16[128,512]{1,0:T(8,128)(2,1)S(1)} %all_gather.9, f32[128,12672]{1,0:T(8,128)} %get-tuple-element.24, f32[128]{0:T(128)S(1)} %get-tuple-element.18, f32[128]{0:T(128)S(1)} %get-tuple-element.17, s32[12672]{0:T(1024)S(1)} %iota_add_fusion, f32[128]{0:T(128)S(1)} %pmax.7, s32[128]{0:T(128)S(1)} %get-tuple-element.12, ...), kind=kOutput, calls=%fused_computation.43 | convolution fusion | flops 1680408576 | bytes 32636800 | tf_op jit(solution)/shard_map/dot_general | solution.py:47
  89.4 0.6 dynamic_slice.3
  90.0 0.0 reduce-scatter.2.cloned.1.call-done
  90.0 0.0 copy-done
  90.0 0.0 copy-done.1
  90.0 1.0 fusion.14
  91.1 1.0 fusion.25
  92.1 0.7 add_convert_fusion
  92.8 6.2 %all-reduce.3 = (f32[512]{0:T(512)}, f32[512]{0:T(512)}) all-reduce(f32[512]{0:T(512)S(1)} %get-tuple-element.8, f32[512]{0:T(512)S(1)} %get-tuple-element.10), channel_id=1, replica_groups=mesh['dp'=2,'tp'=4] {'tp'}, use_global_device_ids=true, to_apply=%region_13.14 | all-reduce | flops 1024 | bytes 8192 | tf_op jit(solution)/shard_map/psum | solution.py:51
  (8 shorter events, 0.1 us)
Async XLA Ops:
  7.2 82.8 %reduce-scatter.2.cloned.1.call-start = ((), (), s32[]{:S(2)}) async-start(), calls=%async_computation.1 | async-start | bytes 327680 | tf_op jit(solution)/shard_map/reduce_scatter | solution.py:49
  70.6 19.4 %copy-start = (bf16[32,512]{1,0:T(8,128)(2,1)S(1)}, bf16[32,512]{1,0:T(8,128)(2,1)}, u32[]{:S(2)}) copy-start(bf16[32,512]{1,0:T(8,128)(2,1)} %param.7) | copy-start | bytes 98308
  70.6 19.4 %copy-start.1 = (f32[512]{0:T(512)S(1)}, f32[512]{0:T(512)}, u32[]{:S(2)}) copy-start(f32[512]{0:T(512)} %param.8) | copy-start | bytes 6148
Sparse Core Ops, SparseCore 0:
  70.7 14.7 reduce-scatter.1
where the time goes:
time: 108 us; the launch traced here: 107 us
  matrix products  39.6 us (37%)
  blocking collectives  33.1 us (31%)
  between operations  17.2 us (16%)
  other arithmetic  13.5 us (12%)
  local copies, waits for them, and re-layouts  3.55 us (3%)
    dot_general x1, matrix products, group_step(): lax.dot_general(d_logits, x_all, (((0,), (0,)), ((), ())), preferred_elem...  17.5 us
    dot_general x1, matrix products, group_step(): lax.dot_general(x_all, out_embed, (((1,), (1,)), ((), ())), preferred_ele...  11.8 us
    dot_general x1, matrix products, group_step(): dx_part = jnp.dot(d_logits, out_embed, preferred_element_type=jnp.float32)  10.3 us
    all_gather x1, blocking collectives, group_step(): lax.all_gather(normed.astype(jnp.bfloat16), 'tp', axis=0, tiled=True)  7.8 us
    unnamed x1, blocking collectives  6.75 us
    psum x1, blocking collectives, group_step(): group_stats = lax.psum(local_stats, 'tp')  6.74 us
    psum x1, blocking collectives, group_step(): d_gain = lax.psum(gain_part, 'tp')  6.2 us
    pmax x1, blocking collectives, group_step(): glob_max = lax.pmax(jnp.max(masked, axis=1), 'tp')  5.63 us
  transfers between devices with their start and end apart: 1, of which 0 were waited for; matrix products, arithmetic and copies ran while one was open for 17% of the time, Pallas kernels for 0%

commit v1 on v0

v1 whole, which is shorter than its diff:
```python
import functools

import jax
import jax.numpy as jnp
from jax import lax
from jax.experimental import pallas as pl
from jax.experimental.pallas import tpu as pltpu
from jax.sharding import PartitionSpec as P

SOFT_CAP = 30.0
Z_COEF = 1e-4
LN_EPS = 1e-5
LOG2E = 1.4426950408889634
MESH = pl.DeviceIdType.MESH
F32 = jnp.float32
BF16 = jnp.bfloat16

TP = 4
TOK = 128
LOC = TOK // TP
DIM = 512
VOCAB = 12672
TILE = 256
GROUP = 7 * TILE
GROUPS = VOCAB // GROUP
TAIL = VOCAB - GROUP * GROUPS
ROWS_B = 1152


def row_sum(val):
    return jnp.sum(val, axis=-1, keepdims=True)


def main_kernel(
    hid_ref, gain_ref, bias_ref, emb_ref, valid_ref, tgt_ref, mask_ref,
    small_ref, dhid_ref, dz_ref, x_ref,
    emb_v, g_v, hid_all, xh_v, rstd_v, meta_v, stat_v, dx_v, dx_recv, gb_v, acc_v,
    emb_sem, send_sem, recv_sem, dz_sem,
):
    me = lax.axis_index("tp")
    dp = lax.axis_index("dp")
    chunks = [(j * GROUP, GROUP) for j in range(GROUPS - 1)]
    chunks.append(((GROUPS - 1) * GROUP, GROUP + TAIL))
    emb_copies = [
        pltpu.make_async_copy(emb_ref.at[pl.ds(s, n), :], emb_v.at[pl.ds(s, n), :], emb_sem.at[k])
        for k, (s, n) in enumerate(chunks)
    ]
    for cp in emb_copies:
        cp.start()

    barrier = pltpu.get_barrier_semaphore()
    for k in range(1, TP):
        pl.semaphore_signal(barrier, inc=1, device_id=(dp, lax.rem(me + k, TP)), device_id_type=MESH)

    lane = lax.broadcasted_iota(jnp.int32, (1, TOK), 1)
    mine = (lane // LOC) == me
    tgt4 = jnp.concatenate([tgt_ref[...]] * TP, axis=1)
    mask4 = jnp.concatenate([mask_ref[...]] * TP, axis=1)
    my_rows = pl.ds(pl.multiple_of(me * LOC, LOC), LOC)
    my_meta = pl.ds(pl.multiple_of(me * 8, 8), 8)
    meta_v[my_meta, :] = jnp.concatenate(
        [jnp.where(mine, tgt4, 0), jnp.where(mine, mask4, 0), jnp.zeros((6, TOK), jnp.int32)], axis=0
    )
    hid_all[my_rows, :] = hid_ref[...]
    pl.semaphore_wait(barrier, TP - 1)

    def push(src, dst, idx):
        copies = []
        for k in range(1, TP):
            cp = pltpu.make_async_remote_copy(
                src_ref=src(k), dst_ref=dst, send_sem=send_sem.at[3 * idx + k - 1], recv_sem=recv_sem.at[3 * idx + k - 1],
                device_id=(dp, lax.rem(me + k, TP)), device_id_type=MESH,
            )
            cp.start()
            copies.append(cp)
        return copies

    first = push(lambda k: hid_ref, hid_all.at[my_rows, :], 0)
    first += push(lambda k: meta_v.at[my_meta, :], meta_v.at[my_meta, :], 1)
    for cp in first:
        cp.wait_recv()

    meta = meta_v[0:8, :] + meta_v[8:16, :] + meta_v[16:24, :] + meta_v[24:32, :]
    tgt_row = meta[0:1, :]
    mask_row = meta[1:2, :].astype(F32)
    tok_count = row_sum(mask_row)
    tgt_col = jnp.transpose(jnp.broadcast_to(tgt_row, (TOK, TOK)))

    h = hid_all[...].astype(F32)
    mean_val = row_sum(h) * (1.0 / DIM)
    cent = h - mean_val
    var_val = row_sum(cent * cent) * (1.0 / DIM)
    rstd = lax.rsqrt(var_val + LN_EPS)
    xh = cent * rstd
    xh_v[...] = xh
    rstd_v[...] = jnp.broadcast_to(rstd, (TOK, TOK))
    x_ref[...] = (xh * gain_ref[...] + bias_ref[...]).astype(BF16)

    col0 = lax.broadcasted_iota(jnp.int32, (TOK, TOK), 1)
    base = me * VOCAB
    tgt_loc = tgt_col - base

    def fwd(start, size):
        z = lax.dot_general(
            x_ref[...], emb_v[pl.ds(start, size), :], (((1,), (1,)), ((), ())), preferred_element_type=F32
        )
        t = jnp.tanh(z * (1.0 / SOFT_CAP))
        ok = valid_ref[:, pl.ds(start, size)].astype(F32)
        e = jnp.exp2(t * (SOFT_CAP * LOG2E)) * ok
        g_v[:, pl.ds(start, size)] = e * (1.0 - t * t)
        s_sum = 0.0
        t_sum = 0.0
        for c in range(size // TOK):
            cols = slice(c * TOK, (c + 1) * TOK)
            s_sum += e[:, cols]
            t_sum += jnp.where(tgt_loc - (start + c * TOK) == col0, t[:, cols], 0.0)
        return s_sum, t_sum

    acc_v[...] = jnp.zeros_like(acc_v)
    for j, (g0, n) in enumerate(chunks):
        emb_copies[j].wait()
        s_acc = 0.0
        t_acc = 0.0
        for s in range(0, n, TILE):
            ds, dt = fwd(g0 + s, min(TILE, n - s))
            s_acc += ds
            t_acc += dt
        acc_v[0] += s_acc
        acc_v[1] += t_acc

    s_loc = jnp.sum(jnp.transpose(acc_v[0]), axis=0, keepdims=True)
    t_loc = jnp.sum(jnp.transpose(acc_v[1]), axis=0, keepdims=True)
    stat_v[my_meta, :] = jnp.concatenate([s_loc, t_loc, jnp.zeros((6, TOK), F32)], axis=0)
    second = push(lambda k: stat_v.at[my_meta, :], stat_v.at[my_meta, :], 2)
    for cp in second:
        cp.wait_recv()
    stats = stat_v[0:8, :] + stat_v[8:16, :] + stat_v[16:24, :] + stat_v[24:32, :]
    sum_exp = stats[0:1, :]
    t_tgt = stats[1:2, :]
    lse = jnp.log(sum_exp)
    loss = (lse - SOFT_CAP * t_tgt + Z_COEF * lse * lse) * mask_row
    mean_loss = row_sum(loss) / tok_count
    coef = mask_row / tok_count
    a_row = (1.0 + 2.0 * Z_COEF * lse) * coef / sum_exp
    c_row = coef * (1.0 - t_tgt * t_tgt)
    a_col = jnp.transpose(jnp.broadcast_to(a_row, (TOK, TOK)))
    c_col = jnp.transpose(jnp.broadcast_to(c_row, (TOK, TOK)))

    def grad(start, size):
        parts = []
        for c in range(size // TOK):
            hit = tgt_loc - (start + c * TOK) == col0
            parts.append(a_col * g_v[:, pl.ds(start + c * TOK, TOK)] - jnp.where(hit, c_col, 0.0))
        return jnp.concatenate(parts, axis=1).astype(BF16)

    dz_copies = []
    for j, (g0, n) in enumerate(chunks):
        dz = grad(g0, n)
        dz_ref[:, pl.ds(g0, n)] = dz
        part = jnp.dot(dz, emb_v[pl.ds(g0, n), :], preferred_element_type=F32)
        dx_v[...] = part if j == 0 else dx_v[...] + part

    dx = dx_v[...]
    gb_v[my_meta, :] = jnp.concatenate(
        [jnp.sum(dx * xh_v[...], axis=0, keepdims=True), jnp.sum(dx, axis=0, keepdims=True), jnp.zeros((6, DIM), F32)], axis=0
    )
    dx_recv[my_rows, :] = dx_v[my_rows, :]

    def peer_rows(k):
        return dx_v.at[pl.ds(pl.multiple_of(lax.rem(me + k, TP) * LOC, LOC), LOC), :]

    third = push(peer_rows, dx_recv.at[my_rows, :], 3)
    third += push(lambda k: gb_v.at[my_meta, :], gb_v.at[my_meta, :], 4)
    for cp in third:
        cp.wait_recv()
    d_norm = dx_recv[0:LOC, :] + dx_recv[LOC:2 * LOC, :] + dx_recv[2 * LOC:3 * LOC, :] + dx_recv[3 * LOC:, :]
    gb = gb_v[0:8, :] + gb_v[8:16, :] + gb_v[16:24, :] + gb_v[24:32, :]
    xh_me = xh_v[my_rows, :]
    dxh = d_norm * gain_ref[...]
    m1 = row_sum(dxh) * (1.0 / DIM)
    m2 = row_sum(dxh * xh_me) * (1.0 / DIM)
    dhid_ref[...] = (rstd_v[my_rows, 0:1] * (dxh - m1 - xh_me * m2)).astype(BF16)
    loss_me = pltpu.roll(loss, lax.rem(TOK - me * LOC, TOK), 1)
    pad = jnp.zeros((1, DIM - TOK), F32)
    small_ref[...] = jnp.concatenate(
        [
            gb[0:2, :],
            jnp.concatenate([loss_me, pad], axis=1),
            jnp.broadcast_to(mean_loss, (1, DIM)),
            jnp.zeros((4, DIM), F32),
        ],
        axis=0,
    )
    for cp in first + second + third:
        cp.wait_send()


def embed_kernel(dz_ref, x_ref, small_ref, dhid_in, demb_ref, tok_ref, mean_ref, dhid_ref, gain_ref, bias_ref):
    demb_ref[...] = lax.dot_general(dz_ref[...], x_ref[...], (((0,), (0,)), ((), ())), preferred_element_type=F32)

    @pl.when(pl.program_id(0) == 0)
    def _():
        gain_ref[...] = small_ref[0:1, :]
        bias_ref[...] = small_ref[1:2, :]
        tok_ref[...] = small_ref[2:3, 0:LOC]
        mean_ref[...] = small_ref[3:4, 0:1]
        dhid_ref[...] = dhid_in[...]


def solution(mesh):
    vmem = pl.BlockSpec(memory_space=pltpu.VMEM)
    hbm = pl.BlockSpec(memory_space=pl.ANY)

    def group_step(hidden, ln_gain, ln_bias, out_embed, vocab_valid, targets, loss_mask):
        small, dhid, dz, x_all = pl.pallas_call(
            main_kernel,
            out_shape=(
                jax.ShapeDtypeStruct((8, DIM), F32),
                jax.ShapeDtypeStruct((LOC, DIM), BF16),
                jax.ShapeDtypeStruct((TOK, VOCAB), BF16),
                jax.ShapeDtypeStruct((TOK, DIM), BF16),
            ),
            in_specs=[vmem, vmem, vmem, hbm, vmem, vmem, vmem],
            out_specs=(vmem, vmem, vmem, vmem),
            scratch_shapes=[
                pltpu.VMEM((VOCAB, DIM), BF16),
                pltpu.VMEM((TOK, VOCAB), F32),
                pltpu.VMEM((TOK, DIM), BF16),
                pltpu.VMEM((TOK, DIM), F32),
                pltpu.VMEM((TOK, TOK), F32),
                pltpu.VMEM((8 * TP, TOK), jnp.int32),
                pltpu.VMEM((8 * TP, TOK), F32),
                pltpu.VMEM((TOK, DIM), F32),
                pltpu.VMEM((TOK, DIM), F32),
                pltpu.VMEM((8 * TP, DIM), F32),
                pltpu.VMEM((2, TOK, TOK), F32),
                pltpu.SemaphoreType.DMA((GROUPS,)),
                pltpu.SemaphoreType.DMA((15,)),
                pltpu.SemaphoreType.DMA((15,)),
                pltpu.SemaphoreType.DMA((GROUPS,)),
            ],
            compiler_params=pltpu.CompilerParams(collective_id=0, has_side_effects=True, vmem_limit_bytes=40 * 1024 * 1024),
            name="main",
        )(
            hidden, ln_gain.reshape(1, DIM), ln_bias.reshape(1, DIM), out_embed, vocab_valid.reshape(1, VOCAB),
            targets.reshape(1, LOC), loss_mask.reshape(1, LOC),
        )
        keep = lambda r, c: pl.BlockSpec((r, c), lambda i: (0, 0))
        d_embed, tok, mean, d_hidden, d_gain, d_bias = pl.pallas_call(
            embed_kernel,
            grid=(VOCAB // ROWS_B,),
            out_shape=(
                jax.ShapeDtypeStruct((VOCAB, DIM), F32),
                jax.ShapeDtypeStruct((1, LOC), F32),
                jax.ShapeDtypeStruct((1, 1), F32),
                jax.ShapeDtypeStruct((LOC, DIM), BF16),
                jax.ShapeDtypeStruct((1, DIM), F32),
                jax.ShapeDtypeStruct((1, DIM), F32),
            ),
            in_specs=[pl.BlockSpec((TOK, ROWS_B), lambda i: (0, i)), keep(TOK, DIM), keep(8, DIM), keep(LOC, DIM)],
            out_specs=(
                pl.BlockSpec((ROWS_B, DIM), lambda i: (i, 0)),
                keep(1, LOC), keep(1, 1), keep(LOC, DIM), keep(1, DIM), keep(1, DIM),
            ),
            compiler_params=pltpu.CompilerParams(vmem_limit_bytes=24 * 1024 * 1024),
            name="embed",
        )(dz, x_all, small, dhid)
        return tok.reshape(LOC), mean.reshape(1), d_hidden, d_embed, d_gain.reshape(DIM), d_bias.reshape(DIM)

    row_spec = P(("dp", "tp"))
    mat_spec = P(("dp", "tp"), None)
    return jax.shard_map(
        group_step, mesh=mesh,
        in_specs=(mat_spec, P(None), P(None), P("tp", None), P("tp"), row_spec, row_spec),
        out_specs=(row_spec, P("dp"), mat_spec, mat_spec, P("dp"), P("dp")), check_vma=False,
    )
```

time: 108 us -> 40.2 us (0.37)
  matrix products: 39.6 us -> 0 us
  Pallas kernels: 0 us -> 35 us
  blocking collectives: 33.1 us -> 0 us
  between operations: 17.2 us -> 0.66 us
  other arithmetic: 13.5 us -> 0 us
    dot_general x3 -> x0, matrix products: 39.6 us -> none  [the longest x1 17.5 us: group_step(): lax.dot_general(d_logits, x_all, (((0,), (0,)), ((), ())), preferred_elem...]
    pallas_call x0 -> x2, Pallas kernels: none -> 35 us  [the longest x1 23.4 us: group_step(): pl.pallas_call(main_kernel, out_shape=(jax.ShapeDtypeStruct((8, DIM), F32...]
    psum x2 -> x0, blocking collectives: 12.9 us -> none  [the longest x1 6.74 us: group_step(): group_stats = lax.psum(local_stats, 'tp')]
    reduce_sum x6 -> x0, other arithmetic: 9.79 us -> none  [the longest x1 5.29 us: group_step(): jnp.sum(exp_vals, axis=1)]
    all_gather x1 -> x0, blocking collectives: 7.8 us -> none  [group_step(): lax.all_gather(normed.astype(jnp.bfloat16), 'tp', axis=0, tiled=True)]
    unnamed x1 -> x0, blocking collectives: 6.75 us -> none
    pmax x1 -> x0, blocking collectives: 5.63 us -> none  [group_step(): glob_max = lax.pmax(jnp.max(masked, axis=1), 'tp')]
    convert_element_type x2 -> x0, other arithmetic: 1.56 us -> none  [the longest x1 0.86 us: group_step(): normed.astype(jnp.bfloat16)]
  transfers between devices with their start and end apart: 1 -> 0, of which waited for: 0 -> 0; matrix products, arithmetic and copies ran while one was open for 17% -> 0% of each run, Pallas kernels for 0% -> 0%
where the time goes in v1:
time: 40.2 us; the launch traced here: 39.9 us
  Pallas kernels  35 us (87%)
  local copies, waits for them, and re-layouts  4.27 us (11%)
  between operations  0.66 us (2%)
    pallas_call x1, Pallas kernels, group_step(): pl.pallas_call(main_kernel, out_shape=(jax.ShapeDtypeStruct((8, DIM), F32...  23.4 us
    pallas_call x1, Pallas kernels, group_step(): pl.pallas_call(embed_kernel, grid=(VOCAB // ROWS_B,), out_shape=(jax.Shap...  11.6 us
    unnamed x10, local copies, waits for them, and re-layouts  3.42 us
    reshape x1, local copies, waits for them, and re-layouts, group_step(): vocab_valid.reshape(1, VOCAB)  0.85 us

profile of v1, /device:TPU:0, one launch (start us, length us, event | category | flops | bytes accessed | tf_op | source)
XLA Modules:
  0.0 39.9 jit_solution(9773594155124033407)
XLA Ops:
  0.6 0.8 %reshape.41.valid_ref = s32[1,12672]{1,0:T(1,128)S(1)} reshape(s32[12672]{0:T(1024)} %param.11) | data formatting | bytes 101376 | tf_op jit(solution)/shard_map/reshape | solution.py:245
  1.5 0.0 copy-start
  1.5 0.7 %copy-done = bf16[32,512]{1,0:T(8,128)(2,1)S(1)} copy-done((bf16[32,512]{1,0:T(8,128)(2,1)S(1)}, bf16[32,512]{1,0:T(8,128)(2,1)}, u32[]{:S(2)}) %copy-start) | copy-done | bytes 32792
  2.2 0.0 copy-start.1
  2.2 0.7 %copy-done.1 = f32[512]{0:T(512)S(1)} copy-done((f32[512]{0:T(512)S(1)}, f32[512]{0:T(512)}, u32[]{:S(2)}) %copy-start.1) | copy-done | bytes 2072
  2.9 0.0 copy-start.2
  2.9 0.7 %copy-done.2 = f32[512]{0:T(512)S(1)} copy-done((f32[512]{0:T(512)S(1)}, f32[512]{0:T(512)}, u32[]{:S(2)}) %copy-start.2) | copy-done | bytes 2072
  3.6 0.0 copy-start.3
  3.6 0.7 %copy-done.3 = s32[32]{0:T(128)S(1)} copy-done((s32[32]{0:T(128)S(1)}, s32[32]{0:T(128)}, u32[]{:S(2)}) %copy-start.3) | copy-done | bytes 152
  4.3 0.0 copy-start.4
  4.3 0.7 %copy-done.4 = s32[32]{0:T(128)S(1)} copy-done((s32[32]{0:T(128)S(1)}, s32[32]{0:T(128)}, u32[]{:S(2)}) %copy-start.4) | copy-done | bytes 152
  4.9 23.4 %main.1 = (f32[8,512]{1,0:T(8,128)S(1)}, bf16[32,512]{1,0:T(8,128)(2,1)S(1)}, bf16[128,12672]{1,0:T(8,128)(2,1)S(1)}, bf16[128,512]{1,0:T(8,128)(2,1)S(1)}) custom-call(bf16[32,512]{1,0:T(8,128)(2,1)S(1)} %copy-done, f32[1,512]{1,0:T(1,128)S(1)} %bitcast.8, f32[1,512]{1,0:T(1,128)S(1)} %bitcast.9, bf16[12672,512]{1,0:T(8,128)(2,1)} %emb_ref.1, ...), custom_call_target="tpu_custom_call" | custom-call | tf_op jit(solution)/shard_map/main/pallas_call | solution.py:215
  28.4 11.6 %embed.1 = (f32[12672,512]{1,0:T(8,128)}, f32[1,32]{1,0:T(1,128)}, f32[1,1]{1,0:T(1,128)}, bf16[32,512]{1,0:T(8,128)(2,1)}, f32[1,512]{1,0:T(1,128)}, /*index=5*/f32[1,512]{1,0:T(1,128)}) custom-call(bf16[128,12672]{1,0:T(8,128)(2,1)S(1)} %get-tuple-element.16.dz_ref, bf16[128,512]{1,0:T(8,128)(2,1)S(1)} %get-tuple-element.17.x_ref, ...), custom_call_target="tpu_custom_call" | custom-call | tf_op jit(solution)/shard_map/embed/pallas_call | solution.py:249
Async XLA Ops:
  1.5 0.8 %copy-start = (bf16[32,512]{1,0:T(8,128)(2,1)S(1)}, bf16[32,512]{1,0:T(8,128)(2,1)}, u32[]{:S(2)}) copy-start(bf16[32,512]{1,0:T(8,128)(2,1)} %hid_ref.1) | copy-start | bytes 98308
  2.2 0.7 %copy-start.1 = (f32[512]{0:T(512)S(1)}, f32[512]{0:T(512)}, u32[]{:S(2)}) copy-start(f32[512]{0:T(512)} %param.8) | copy-start | bytes 6148
  2.9 0.7 %copy-start.2 = (f32[512]{0:T(512)S(1)}, f32[512]{0:T(512)}, u32[]{:S(2)}) copy-start(f32[512]{0:T(512)} %param.9) | copy-start | bytes 6148
  3.6 0.7 %copy-start.3 = (s32[32]{0:T(128)S(1)}, s32[32]{0:T(128)}, u32[]{:S(2)}) copy-start(s32[32]{0:T(128)} %param.12) | copy-start | bytes 388
  4.3 0.7 %copy-start.4 = (s32[32]{0:T(128)S(1)}, s32[32]{0:T(128)}, u32[]{:S(2)}) copy-start(s32[32]{0:T(128)} %param.13) | copy-start | bytes 388

commit v2 on v1

--- a/solution.py
+++ b/solution.py
@@ -24,7 +24,6 @@
 GROUP = 7 * TILE
 GROUPS = VOCAB // GROUP
 TAIL = VOCAB - GROUP * GROUPS
-ROWS_B = 1152
 
 
 def row_sum(val):
@@ -32,13 +31,23 @@
 
 
 def main_kernel(
-    hid_ref, gain_ref, bias_ref, emb_ref, valid_ref, tgt_ref, mask_ref,
+    hid_hbm, gain_hbm, bias_hbm, emb_ref, valid_hbm, tgt_hbm, mask_hbm,
     small_ref, dhid_ref, dz_ref, x_ref,
+    hid_ref, gain_ref, bias_ref, valid_ref, tgt_ref, mask_ref,
     emb_v, g_v, hid_all, xh_v, rstd_v, meta_v, stat_v, dx_v, dx_recv, gb_v, acc_v,
-    emb_sem, send_sem, recv_sem, dz_sem,
+    emb_sem, send_sem, recv_sem, in_sem,
 ):
     me = lax.axis_index("tp")
     dp = lax.axis_index("dp")
+    ins = [
+        pltpu.make_async_copy(src, dst, in_sem.at[k])
+        for k, (src, dst) in enumerate([
+            (hid_hbm, hid_ref), (tgt_hbm, tgt_ref), (mask_hbm, mask_ref),
+            (gain_hbm, gain_ref), (bias_hbm, bias_ref), (valid_hbm, valid_ref),
+        ])
+    ]
+    for cp in ins:
+        cp.start()
     chunks = [(j * GROUP, GROUP) for j in range(GROUPS - 1)]
     chunks.append(((GROUPS - 1) * GROUP, GROUP + TAIL))
     emb_copies = [
@@ -52,6 +61,8 @@
     for k in range(1, TP):
         pl.semaphore_signal(barrier, inc=1, device_id=(dp, lax.rem(me + k, TP)), device_id_type=MESH)
 
+    for cp in ins[:3]:
+        cp.wait()
     lane = lax.broadcasted_iota(jnp.int32, (1, TOK), 1)
     mine = (lane // LOC) == me
     tgt4 = jnp.concatenate([tgt_ref[...]] * TP, axis=1)
@@ -77,6 +88,8 @@
 
     first = push(lambda k: hid_ref, hid_all.at[my_rows, :], 0)
     first += push(lambda k: meta_v.at[my_meta, :], meta_v.at[my_meta, :], 1)
+    for cp in ins[3:]:
+        cp.wait()
     for cp in first:
         cp.wait_recv()
 
@@ -105,8 +118,8 @@
             x_ref[...], emb_v[pl.ds(start, size), :], (((1,), (1,)), ((), ())), preferred_element_type=F32
         )
         t = jnp.tanh(z * (1.0 / SOFT_CAP))
-        ok = valid_ref[:, pl.ds(start, size)].astype(F32)
-        e = jnp.exp2(t * (SOFT_CAP * LOG2E)) * ok
+        ok = jnp.concatenate([valid_ref[c:c + 1, :] for c in range(start // TOK, (start + size) // TOK)], axis=1)
+        e = jnp.exp2(t * (SOFT_CAP * LOG2E)) * ok.astype(F32)
         g_v[:, pl.ds(start, size)] = e * (1.0 - t * t)
         s_sum = 0.0
         t_sum = 0.0
@@ -195,21 +208,33 @@
         cp.wait_send()
 
 
-def embed_kernel(dz_ref, x_ref, small_ref, dhid_in, demb_ref, tok_ref, mean_ref, dhid_ref, gain_ref, bias_ref):
-    demb_ref[...] = lax.dot_general(dz_ref[...], x_ref[...], (((0,), (0,)), ((), ())), preferred_element_type=F32)
-
-    @pl.when(pl.program_id(0) == 0)
-    def _():
-        gain_ref[...] = small_ref[0:1, :]
-        bias_ref[...] = small_ref[1:2, :]
-        tok_ref[...] = small_ref[2:3, 0:LOC]
-        mean_ref[...] = small_ref[3:4, 0:1]
-        dhid_ref[...] = dhid_in[...]
+OUT_TILES = [384] + [768] * 16
+
+
+def embed_kernel(dz_ref, x_ref, small_ref, dhid_in, demb_ref, tok_ref, mean_ref, dhid_ref, gain_ref, bias_ref, stage, out_sem):
+    copies = []
+    start = 0
+    for k, n in enumerate(OUT_TILES):
+        rows = pl.ds(start, n)
+        stage[rows, :] = lax.dot_general(
+            dz_ref[:, rows], x_ref[...], (((0,), (0,)), ((), ())), preferred_element_type=F32
+        )
+        cp = pltpu.make_async_copy(stage.at[rows, :], demb_ref.at[rows, :], out_sem.at[k])
+        cp.start()
+        copies.append(cp)
+        start += n
+    gain_ref[...] = small_ref[0:1, :]
+    bias_ref[...] = small_ref[1:2, :]
+    tok_ref[...] = small_ref[2:3, 0:LOC]
+    mean_ref[...] = small_ref[3:4, 0:1]
+    dhid_ref[...] = dhid_in[...]
+    for cp in copies:
+        cp.wait()
 
 
 def solution(mesh):
     vmem = pl.BlockSpec(memory_space=pltpu.VMEM)
-    hbm = pl.BlockSpec(memory_space=pl.ANY)
+    hbm = pl.BlockSpec(memory_space=pltpu.HBM)
 
     def group_step(hidden, ln_gain, ln_bias, out_embed, vocab_valid, targets, loss_mask):
         small, dhid, dz, x_all = pl.pallas_call(
@@ -220,9 +245,15 @@
                 jax.ShapeDtypeStruct((TOK, VOCAB), BF16),
                 jax.ShapeDtypeStruct((TOK, DIM), BF16),
             ),
-            in_specs=[vmem, vmem, vmem, hbm, vmem, vmem, vmem],
+            in_specs=[hbm] * 7,
             out_specs=(vmem, vmem, vmem, vmem),
             scratch_shapes=[
+                pltpu.VMEM((LOC, DIM), BF16),
+                pltpu.VMEM((1, DIM), F32),
+                pltpu.VMEM((1, DIM), F32),
+                pltpu.VMEM((VOCAB // TOK, TOK), jnp.int32),
+                pltpu.VMEM((1, LOC), jnp.int32),
+                pltpu.VMEM((1, LOC), jnp.int32),
                 pltpu.VMEM((VOCAB, DIM), BF16),
                 pltpu.VMEM((TOK, VOCAB), F32),
                 pltpu.VMEM((TOK, DIM), BF16),
@@ -237,18 +268,21 @@
                 pltpu.SemaphoreType.DMA((GROUPS,)),
                 pltpu.SemaphoreType.DMA((15,)),
                 pltpu.SemaphoreType.DMA((15,)),
-                pltpu.SemaphoreType.DMA((GROUPS,)),
+                pltpu.SemaphoreType.DMA((6,)),
             ],
             compiler_params=pltpu.CompilerParams(collective_id=0, has_side_effects=True, vmem_limit_bytes=40 * 1024 * 1024),
             name="main",
         )(
-            hidden, ln_gain.reshape(1, DIM), ln_bias.reshape(1, DIM), out_embed, vocab_valid.reshape(1, VOCAB),
-            targets.reshape(1, LOC), loss_mask.reshape(1, LOC),
+            *(
+                pltpu.with_memory_space_constraint(val, pltpu.HBM)
+                for val in (
+                    hidden, ln_gain.reshape(1, DIM), ln_bias.reshape(1, DIM), out_embed,
+                    vocab_valid.reshape(VOCAB // TOK, TOK), targets.reshape(1, LOC), loss_mask.reshape(1, LOC),
+                )
+            )
         )
-        keep = lambda r, c: pl.BlockSpec((r, c), lambda i: (0, 0))
         d_embed, tok, mean, d_hidden, d_gain, d_bias = pl.pallas_call(
             embed_kernel,
-            grid=(VOCAB // ROWS_B,),
             out_shape=(
                 jax.ShapeDtypeStruct((VOCAB, DIM), F32),
                 jax.ShapeDtypeStruct((1, LOC), F32),
@@ -257,12 +291,10 @@
                 jax.ShapeDtypeStruct((1, DIM), F32),
                 jax.ShapeDtypeStruct((1, DIM), F32),
             ),
-            in_specs=[pl.BlockSpec((TOK, ROWS_B), lambda i: (0, i)), keep(TOK, DIM), keep(8, DIM), keep(LOC, DIM)],
-            out_specs=(
-                pl.BlockSpec((ROWS_B, DIM), lambda i: (i, 0)),
-                keep(1, LOC), keep(1, 1), keep(LOC, DIM), keep(1, DIM), keep(1, DIM),
-            ),
-            compiler_params=pltpu.CompilerParams(vmem_limit_bytes=24 * 1024 * 1024),
+            in_specs=[vmem] * 4,
+            out_specs=(hbm, vmem, vmem, vmem, vmem, vmem),
+            scratch_shapes=[pltpu.VMEM((VOCAB, DIM), F32), pltpu.SemaphoreType.DMA((len(OUT_TILES),))],
+            compiler_params=pltpu.CompilerParams(vmem_limit_bytes=36 * 1024 * 1024),
             name="embed",
         )(dz, x_all, small, dhid)
         return tok.reshape(LOC), mean.reshape(1), d_hidden, d_embed, d_gain.reshape(DIM), d_bias.reshape(DIM)

time: 40.2 us -> 35.6 us (0.89)
  local copies, waits for them, and re-layouts: 4.27 us -> 0 us
    unnamed x10 -> x0, local copies, waits for them, and re-layouts: 3.42 us -> none
    pallas_call x1, Pallas kernels: 11.6 us -> 9.69 us  [group_step(): pl.pallas_call(embed_kernel, out_shape=(jax.ShapeDtypeStruct((VOCAB, DIM)...]
    pallas_call x1, Pallas kernels: 23.4 us -> 25.2 us  [group_step(): pl.pallas_call(main_kernel, out_shape=(jax.ShapeDtypeStruct((8, DIM), F32...]
    reshape x1 -> x0, local copies, waits for them, and re-layouts: 0.85 us -> none  [group_step(): vocab_valid.reshape(1, VOCAB)]
where the time goes in v2:
time: 35.6 us; the launch traced here: 35.5 us
  Pallas kernels  34.9 us (98%)
  between operations  0.64 us (2%)
    pallas_call x1, Pallas kernels, group_step(): pl.pallas_call(main_kernel, out_shape=(jax.ShapeDtypeStruct((8, DIM), F32...  25.2 us
    pallas_call x1, Pallas kernels, group_step(): pl.pallas_call(embed_kernel, out_shape=(jax.ShapeDtypeStruct((VOCAB, DIM)...  9.69 us

profile of v2, /device:TPU:0, one launch (start us, length us, event | category | flops | bytes accessed | tf_op | source)
XLA Modules:
  0.0 35.5 jit_solution(14616084681582516013)
XLA Ops:
  0.6 25.2 %main.1 = (f32[8,512]{1,0:T(8,128)S(1)}, bf16[32,512]{1,0:T(8,128)(2,1)S(1)}, bf16[128,12672]{1,0:T(8,128)(2,1)S(1)}, bf16[128,512]{1,0:T(8,128)(2,1)S(1)}) custom-call(bf16[32,512]{1,0:T(8,128)(2,1)} %hid_hbm.1, f32[1,512]{1,0:T(1,128)} %bitcast.10, f32[1,512]{1,0:T(1,128)} %bitcast.11, bf16[12672,512]{1,0:T(8,128)(2,1)} %emb_ref.1, s32[99,128]{1,0:T(8,128)} %bitcast.9, ...), custom_call_target="tpu_custom_call" | custom-call | tf_op jit(solution)/shard_map/main/pallas_call | solution.py:240
  25.8 9.7 %embed.1 = (f32[12672,512]{1,0:T(8,128)}, f32[1,32]{1,0:T(1,128)}, f32[1,1]{1,0:T(1,128)}, bf16[32,512]{1,0:T(8,128)(2,1)}, f32[1,512]{1,0:T(1,128)}, /*index=5*/f32[1,512]{1,0:T(1,128)}) custom-call(bf16[128,12672]{1,0:T(8,128)(2,1)S(1)} %get-tuple-element.16.dz_ref, bf16[128,512]{1,0:T(8,128)(2,1)S(1)} %get-tuple-element.17.x_ref, ...), custom_call_target="tpu_custom_call" | custom-call | tf_op jit(solution)/shard_map/embed/pallas_call | solution.py:284
